TPU v7x, 32 devices: a whole 2x2x4 slice. The times are simulated.
32 devices in a mesh: chrom: 2 (over y), var: 16 (over z, x, core).
Axes of the slice: x: 2, y: 2, z: 4, core: 2. Of those that a mesh axis runs over, the one named last changes fastest.
Arguments:
- genotypes: bfloat16 [2048, 16384], P(None, ('chrom', 'var')), parts along dimension 1, may hold values from -6 to 6
- weights: float32 [512, 32, 3072], P(('chrom', 'var')), parts along dimension 0, may hold values from -0.109375 to 0.109375
- starts: int32 [512], P(('chrom', 'var')), parts along dimension 0, may hold values from 0 to 8191, as said below
- ends: int32 [512], P(('chrom', 'var')), parts along dimension 0, may hold values from 1 to 8192, as said below
- phenotypes: float32 [2048, 32], replicated, may hold values from -6 to 6
Outputs:
- scores: float32 [512, 1024], P(('chrom', 'var')), parts along dimension 0
- linkage: bfloat16 [16384, 1536], P(('chrom', 'var')), parts along dimension 0
There are 2 independent parts, one for each index of `chrom`. A program takes and returns all parts, laid end to end along the dimension named above; an argument that names none is the same for every part. Nothing has to cross between parts.
Inputs may be any that keep to these rules, and one draw needn't show every extreme that they name: starts[g] lies between (g // 16) * 512 and (g // 16) * 512 + 511. ends[g] - starts[g] is between 1 and 3072, equals 3072 for gene 0, and ends[g] <= 8192.
All inputs are finite; a program needn't handle non-finite values.
Results may differ from a plain program's by a relative error of at most 0.0057.
Values may be sent and summed in bfloat16 or wider, within the bound.
A program may use at most 128 MiB of HBM per device.

v0:
```python
import jax
import jax.numpy as jnp
from jax import lax
from jax.sharding import PartitionSpec as P

EPSILON = 1e-05


def from_behind(value, axis, steps):
    count = lax.axis_size(axis)
    first, last = (max(0, -steps), min(count, count - steps))
    return lax.ppermute(value, axis, [(source, source + steps) for source in range(first, last)])


def padded_2(block, sides, width):
    for axis, dim in sides:
        count = lax.axis_size(axis)
        forward = [(i, i + 1) for i in range(count - 1)]
        backward = [(target, source) for source, target in forward]
        low = lax.ppermute(
            lax.slice_in_dim(block, block.shape[dim] - width, None, axis=dim), axis, forward
        )
        high = lax.ppermute(lax.slice_in_dim(block, 0, width, axis=dim), axis, backward)
        block = jnp.concatenate([low, block, high], axis=dim)
    return block


def standardize(values):
    centre = jnp.mean(values, axis=0)
    centred = values - centre
    spread = jnp.mean(centred * centred, axis=0)
    return (centred * lax.rsqrt(spread + EPSILON)).astype(jnp.bfloat16)


def place_weights(gene_weights, gene_starts, gene_ends, anchor, window_cols):
    span = gene_weights.shape[2]
    column = jnp.arange(span, dtype=jnp.int32)
    lengths = gene_ends - gene_starts
    rounded = gene_weights.astype(jnp.bfloat16)
    masked = jnp.where(
        column[None, None, :] < lengths[:, None, None], rounded, jnp.zeros_like(rounded)
    )
    padded = jnp.pad(masked, ((0, 0), (0, 0), (window_cols, window_cols - span)))
    offsets = gene_starts - anchor

    def place_one(single, offset):
        return lax.dynamic_slice_in_dim(single, window_cols - offset, window_cols, 1)

    placed = jax.vmap(place_one)(padded, offsets)
    return placed.reshape(-1, window_cols)


def cross_product(left, right):
    return lax.dot_general(
        left, right, (((0,), (0,)), ((), ())), preferred_element_type=jnp.float32
    )


def on_device(genotypes, weights, starts, ends, phenotypes):
    samples, block_cols = genotypes.shape
    reach_blocks = weights.shape[2] // block_cols
    window_cols = (reach_blocks + 1) * block_cols
    anchor = lax.axis_index("var") * block_cols
    placed = place_weights(weights, starts, ends, anchor, window_cols)

    def add_block(running, incoming, distance):
        weight_slab = placed[:, distance * block_cols : (distance + 1) * block_cols]
        return running + lax.dot_general(
            incoming, weight_slab, (((1,), (1,)), ((), ())), preferred_element_type=jnp.float32
        )

    expression = jnp.zeros((samples, placed.shape[0]), jnp.float32)
    expression = add_block(expression, genotypes, 0)
    incoming = genotypes
    for distance in range(1, reach_blocks + 1):
        incoming = from_behind(incoming, "var", -1)
        expression = add_block(expression, incoming, distance)
    scaled = standardize(expression)
    pheno_scaled = standardize(phenotypes)
    scores = cross_product(scaled, pheno_scaled) / jnp.sqrt(jnp.float32(samples))
    scores = scores.reshape(weights.shape[0], -1)
    gene_cols = scaled.shape[1]
    beside_all = padded_2(scaled, (("var", 1),), gene_cols)
    linkage = (cross_product(scaled, beside_all) / jnp.float32(samples)).astype(jnp.bfloat16)
    return (scores, linkage)


def solution(mesh):
    placed = (
        P(None, ("chrom", "var")),
        P(("chrom", "var"), None, None),
        P(("chrom", "var")),
        P(("chrom", "var")),
        P(),
    )
    return jax.shard_map(
        on_device,
        mesh=mesh,
        in_specs=placed,
        out_specs=(P(("chrom", "var"), None), P(("chrom", "var"), None)),
        check_vma=False,
    )
```

profile of v0, /device:TPU:18, one launch (start us, length us, event | category | flops | bytes accessed | tf_op | source)
XLA Modules:
  0.0 274.0 jit_solution(4751779739847061258)
XLA Ops:
  2.6 23.8 %collective-permute-done = bf16[2048,512]{1,0:T(8,128)(2,1)S(1)} collective-permute-done((bf16[2048,512]{1,0:T(8,128)(2,1)}, bf16[2048,512]{1,0:T(8,128)(2,1)S(1)}, u32[]{:S(2)}, u32[]{:S(2)}) %collective-permute-start) | collective-permute-done | bytes 2097184 | tf_op jit(solution)/shard_map/ppermute | solution.py:12
  27.8 3.7 %collective-permute-start.1 = (bf16[2048,512]{1,0:T(8,128)(2,1)S(1)}, bf16[2048,512]{1,0:T(8,128)(2,1)S(1)}, u32[]{:S(2)}, u32[]{:S(2)}) collective-permute-start(bf16[2048,512]{1,0:T(8,128)(2,1)S(1)} %collective-permute-done), channel_id=1, source_target_pairs={{1,0},{2,1},{3,2},{4,3},{5,4},{6,5},{7,6},{8,7},{9,8},{10,9},{11,1... | collective-permute-start | bytes 6291464 | tf_op jit(solution)/shard_map/ppermute | solution.py:12
  31.5 23.5 %collective-permute-done.1 = bf16[2048,512]{1,0:T(8,128)(2,1)S(1)} collective-permute-done((bf16[2048,512]{1,0:T(8,128)(2,1)S(1)}, bf16[2048,512]{1,0:T(8,128)(2,1)S(1)}, u32[]{:S(2)}, u32[]{:S(2)}) %collective-permute-start.1) | collective-permute-done | bytes 2097184 | tf_op jit(solution)/shard_map/ppermute | solution.py:12
  56.3 3.8 %collective-permute-start.2 = (bf16[2048,512]{1,0:T(8,128)(2,1)S(1)}, bf16[2048,512]{1,0:T(8,128)(2,1)S(1)}, u32[]{:S(2)}, u32[]{:S(2)}) collective-permute-start(bf16[2048,512]{1,0:T(8,128)(2,1)S(1)} %collective-permute-done.1), channel_id=1, source_target_pairs={{1,0},{2,1},{3,2},{4,3},{5,4},{6,5},{7,6},{8,7},{9,8},{10,9},{11,1... | collective-permute-start | bytes 6291464 | tf_op jit(solution)/shard_map/ppermute | solution.py:12
  60.1 23.5 %collective-permute-done.2 = bf16[2048,512]{1,0:T(8,128)(2,1)S(1)} collective-permute-done((bf16[2048,512]{1,0:T(8,128)(2,1)S(1)}, bf16[2048,512]{1,0:T(8,128)(2,1)S(1)}, u32[]{:S(2)}, u32[]{:S(2)}) %collective-permute-start.2) | collective-permute-done | bytes 2097184 | tf_op jit(solution)/shard_map/ppermute | solution.py:12
  83.7 3.8 %collective-permute-start.3 = (bf16[2048,512]{1,0:T(8,128)(2,1)S(1)}, bf16[2048,512]{1,0:T(8,128)(2,1)}, u32[]{:S(2)}, u32[]{:S(2)}) collective-permute-start(bf16[2048,512]{1,0:T(8,128)(2,1)S(1)} %collective-permute-done.2), channel_id=1, source_target_pairs={{1,0},{2,1},{3,2},{4,3},{5,4},{6,5},{7,6},{8,7},{9,8},{10,9},{11,1... | collective-permute-start | bytes 6291464 | tf_op jit(solution)/shard_map/ppermute | solution.py:12
  88.3 3.2 %convert_select_fusion = bf16[16,32,3072]{2,1,0:T(8,128)(2,1)S(1)} fusion(f32[16,32,3072]{2,1,0:T(8,128)} %param.6, pred[16,3072]{1,0:T(8,128)(4,1)S(1)} %iota_compare_fusion), kind=kLoop, calls=%fused_computation.12 | loop fusion | flops 3145728 | bytes 9486336 | tf_op jit(solution)/shard_map/jit(_where)/select_n | solution.py:40
  91.5 3.8 %pad.5 = bf16[16,32,7168]{2,1,0:T(8,128)(2,1)} pad(bf16[16,32,3072]{2,1,0:T(8,128)(2,1)S(1)} %convert_select_fusion, bf16[]{:T(256)} %constant.10.clone.1), padding=0_0x0_0x3584_512 | pad | bytes 10485762 | tf_op jit(solution)/shard_map/jit(_pad)/pad | solution.py:43
  95.3 15.7 %collective-permute-done.3 = bf16[2048,512]{1,0:T(8,128)(2,1)} collective-permute-done((bf16[2048,512]{1,0:T(8,128)(2,1)S(1)}, bf16[2048,512]{1,0:T(8,128)(2,1)}, u32[]{:S(2)}, u32[]{:S(2)}) %collective-permute-start.3) | collective-permute-done | bytes 2097184 | tf_op jit(solution)/shard_map/ppermute | solution.py:12
  111.0 3.9 %collective-permute-start.4 = (bf16[2048,512]{1,0:T(8,128)(2,1)}, bf16[2048,512]{1,0:T(8,128)(2,1)}, u32[]{:S(2)}, u32[]{:S(2)}) collective-permute-start(bf16[2048,512]{1,0:T(8,128)(2,1)} %collective-permute-done.3), channel_id=1, source_target_pairs={{1,0},{2,1},{3,2},{4,3},{5,4},{6,5},{7,6},{8,7},{9,8},{10,9},{11,1... | collective-permute-start | bytes 6291464 | tf_op jit(solution)/shard_map/ppermute | solution.py:12
  114.9 59.9 %while.1 = (s32[]{:T(128)}, bf16[16,32,7168]{2,1,0:T(8,128)(2,1)}, s32[16,3]{0,1:T(4,128)S(1)}, bf16[16,32,3584]{2,1,0:T(8,128)(2,1)}, s32[]{:T(128)}) while((s32[]{:T(128)}, bf16[16,32,7168]{2,1,0:T(8,128)(2,1)}, s32[16,3]{0,1:T(4,128)S(1)}, bf16[16,32,3584]{2,1,0:T(8,128)(2,1)}, s32[]{:T(128)}) %tuple.25), condition=%wide.while_cond, body=%wide.while_body.sunk | while | flops 2 | bytes 459893 | solution.py:47
  115.6 3.1 %dynamic-slice_dynamic-update-slice_fusion.2 = bf16[16,32,3584]{2,1,0:T(8,128)(2,1)} fusion(bf16[16,32,3584]{2,1,0:T(8,128)(2,1)} %get-tuple-element.61, s32[]{:T(128)S(6)} %copy.11, bf16[16,32,7168]{2,1,0:T(8,128)(2,1)} %get-tuple-element.64, s32[]{:T(128)} %bitcast.18, s32[]{:T(128)} %bitcast.19), kind=kLoop, calls=%fused_computation.clone.1 | loop fusion | bytes 459780 | tf_op jit(solution)/shard_map/vmap()/gather
  119.3 3.1 %dynamic-slice_dynamic-update-slice_fusion.2 = bf16[16,32,3584]{2,1,0:T(8,128)(2,1)} fusion(bf16[16,32,3584]{2,1,0:T(8,128)(2,1)} %get-tuple-element.61, s32[]{:T(128)S(6)} %copy.11, bf16[16,32,7168]{2,1,0:T(8,128)(2,1)} %get-tuple-element.64, s32[]{:T(128)} %bitcast.18, s32[]{:T(128)} %bitcast.19), kind=kLoop, calls=%fused_computation.clone.1 | loop fusion | bytes 459780 | tf_op jit(solution)/shard_map/vmap()/gather
  130.5 3.1 %dynamic-slice_dynamic-update-slice_fusion.2 = bf16[16,32,3584]{2,1,0:T(8,128)(2,1)} fusion(bf16[16,32,3584]{2,1,0:T(8,128)(2,1)} %get-tuple-element.61, s32[]{:T(128)S(6)} %copy.11, bf16[16,32,7168]{2,1,0:T(8,128)(2,1)} %get-tuple-element.64, s32[]{:T(128)} %bitcast.18, s32[]{:T(128)} %bitcast.19), kind=kLoop, calls=%fused_computation.clone.1 | loop fusion | bytes 459780 | tf_op jit(solution)/shard_map/vmap()/gather
  134.3 3.1 %dynamic-slice_dynamic-update-slice_fusion.2 = bf16[16,32,3584]{2,1,0:T(8,128)(2,1)} fusion(bf16[16,32,3584]{2,1,0:T(8,128)(2,1)} %get-tuple-element.61, s32[]{:T(128)S(6)} %copy.11, bf16[16,32,7168]{2,1,0:T(8,128)(2,1)} %get-tuple-element.64, s32[]{:T(128)} %bitcast.18, s32[]{:T(128)} %bitcast.19), kind=kLoop, calls=%fused_computation.clone.1 | loop fusion | bytes 459780 | tf_op jit(solution)/shard_map/vmap()/gather
  145.5 3.1 %dynamic-slice_dynamic-update-slice_fusion.2 = bf16[16,32,3584]{2,1,0:T(8,128)(2,1)} fusion(bf16[16,32,3584]{2,1,0:T(8,128)(2,1)} %get-tuple-element.61, s32[]{:T(128)S(6)} %copy.11, bf16[16,32,7168]{2,1,0:T(8,128)(2,1)} %get-tuple-element.64, s32[]{:T(128)} %bitcast.18, s32[]{:T(128)} %bitcast.19), kind=kLoop, calls=%fused_computation.clone.1 | loop fusion | bytes 459780 | tf_op jit(solution)/shard_map/vmap()/gather
  156.7 3.1 %dynamic-slice_dynamic-update-slice_fusion.2 = bf16[16,32,3584]{2,1,0:T(8,128)(2,1)} fusion(bf16[16,32,3584]{2,1,0:T(8,128)(2,1)} %get-tuple-element.61, s32[]{:T(128)S(6)} %copy.11, bf16[16,32,7168]{2,1,0:T(8,128)(2,1)} %get-tuple-element.64, s32[]{:T(128)} %bitcast.18, s32[]{:T(128)} %bitcast.19), kind=kLoop, calls=%fused_computation.clone.1 | loop fusion | bytes 459780 | tf_op jit(solution)/shard_map/vmap()/gather
  160.4 3.1 %dynamic-slice_dynamic-update-slice_fusion.2 = bf16[16,32,3584]{2,1,0:T(8,128)(2,1)} fusion(bf16[16,32,3584]{2,1,0:T(8,128)(2,1)} %get-tuple-element.61, s32[]{:T(128)S(6)} %copy.11, bf16[16,32,7168]{2,1,0:T(8,128)(2,1)} %get-tuple-element.64, s32[]{:T(128)} %bitcast.18, s32[]{:T(128)} %bitcast.19), kind=kLoop, calls=%fused_computation.clone.1 | loop fusion | bytes 459780 | tf_op jit(solution)/shard_map/vmap()/gather
  164.2 3.1 %dynamic-slice_dynamic-update-slice_fusion.2 = bf16[16,32,3584]{2,1,0:T(8,128)(2,1)} fusion(bf16[16,32,3584]{2,1,0:T(8,128)(2,1)} %get-tuple-element.61, s32[]{:T(128)S(6)} %copy.11, bf16[16,32,7168]{2,1,0:T(8,128)(2,1)} %get-tuple-element.64, s32[]{:T(128)} %bitcast.18, s32[]{:T(128)} %bitcast.19), kind=kLoop, calls=%fused_computation.clone.1 | loop fusion | bytes 459780 | tf_op jit(solution)/shard_map/vmap()/gather
  168.0 3.1 %dynamic-slice_dynamic-update-slice_fusion.2 = bf16[16,32,3584]{2,1,0:T(8,128)(2,1)} fusion(bf16[16,32,3584]{2,1,0:T(8,128)(2,1)} %get-tuple-element.61, s32[]{:T(128)S(6)} %copy.11, bf16[16,32,7168]{2,1,0:T(8,128)(2,1)} %get-tuple-element.64, s32[]{:T(128)} %bitcast.18, s32[]{:T(128)} %bitcast.19), kind=kLoop, calls=%fused_computation.clone.1 | loop fusion | bytes 459780 | tf_op jit(solution)/shard_map/vmap()/gather
  174.8 4.0 %collective-permute-start.5 = (bf16[2048,512]{1,0:T(8,128)(2,1)}, bf16[2048,512]{1,0:T(8,128)(2,1)S(1)}, u32[]{:S(2)}, u32[]{:S(2)}) collective-permute-start(bf16[2048,512]{1,0:T(8,128)(2,1)} %collective-permute-done.4), channel_id=1, source_target_pairs={{1,0},{2,1},{3,2},{4,3},{5,4},{6,5},{7,6},{8,7},{9,8},{10,9},{11,1... | collective-permute-start | bytes 6291464 | tf_op jit(solution)/shard_map/ppermute | solution.py:12
  178.9 3.2 %fusion.23 = f32[512,2048]{1,0:T(8,128)S(1)} fusion(bf16[2048,512]{1,0:T(8,128)(2,1)} %param.5, bf16[512,3584]{1,0:T(8,128)(2,1)} %bitcast.20), kind=kOutput, calls=%fused_computation.26 | convolution fusion | flops 1073741824 | bytes 6815744 | tf_op jit(solution)/shard_map/dot_general | solution.py:68
  185.5 3.2 %fusion.17 = f32[512,2048]{1,0:T(8,128)} fusion(bf16[2048,512]{1,0:T(8,128)(2,1)S(1)} %copy-done.8, bf16[512,3584]{1,0:T(8,128)(2,1)S(1)} %bitcast.24), kind=kOutput, calls=%fused_computation.20 | convolution fusion | flops 1073741824 | bytes 6815744 | tf_op jit(solution)/shard_map/dot_general | solution.py:68
  188.8 4.9 %fusion.15 = f32[512,2048]{1,0:T(8,128)} fusion(bf16[2048,512]{1,0:T(8,128)(2,1)} %collective-permute-done.3, bf16[512,3584]{1,0:T(8,128)(2,1)S(1)} %bitcast.25), kind=kOutput, calls=%fused_computation.18 | convolution fusion | flops 1073741824 | bytes 6815744 | tf_op jit(solution)/shard_map/dot_general | solution.py:68
  193.6 4.8 %fusion.13 = f32[512,2048]{1,0:T(8,128)} fusion(bf16[2048,512]{1,0:T(8,128)(2,1)} %collective-permute-done.4, bf16[512,3584]{1,0:T(8,128)(2,1)S(1)} %bitcast.26), kind=kOutput, calls=%fused_computation.16 | convolution fusion | flops 1073741824 | bytes 6815744 | tf_op jit(solution)/shard_map/dot_general | solution.py:68
  198.5 4.2 %collective-permute-done.5 = bf16[2048,512]{1,0:T(8,128)(2,1)S(1)} collective-permute-done((bf16[2048,512]{1,0:T(8,128)(2,1)}, bf16[2048,512]{1,0:T(8,128)(2,1)S(1)}, u32[]{:S(2)}, u32[]{:S(2)}) %collective-permute-start.5) | collective-permute-done | bytes 2097184 | tf_op jit(solution)/shard_map/ppermute | solution.py:12
  202.7 7.3 %fusion.30 = (f32[512]{0:T(512)S(1)}, f32[512,2048]{1,0:T(8,128)S(1)}) fusion(bf16[2048,512]{1,0:T(8,128)(2,1)S(1)} %collective-permute-done.5, bf16[512,3584]{1,0:T(8,128)(2,1)} %bitcast.21, f32[512,2048]{1,0:T(8,128)} %fusion.13, f32[512,2048]{1,0:T(8,128)} %fusion.15, f32[512,2048]{1,0:T(8,128)} %fusion.17, f32[512,2048]{1,0:T(8,128)S(1)} %fusion.19, ...), kind=kOutput, calls=%fused_computation.42 | convolution fusion | flops 1081081344 | bytes 31983616 | tf_op jit(solution)/shard_map/dot_general | solution.py:68
  212.7 3.7 %collective-permute-start.7 = (bf16[2048,512]{0,1:T(8,128)(2,1)}, bf16[2048,512]{0,1:T(8,128)(2,1)}, u32[]{:S(2)}, u32[]{:S(2)}) collective-permute-start(bf16[2048,512]{0,1:T(8,128)(2,1)} %fusion.40), channel_id=1, source_target_pairs={{1,0},{2,1},{3,2},{4,3},{5,4},{6,5},{7,6},{8,7},{9,8},{10,9},{11,1... | collective-permute-start | bytes 6291464 | tf_op jit(solution)/shard_map/ppermute | solution.py:23
  216.4 4.3 %collective-permute-start.6 = (bf16[2048,512]{0,1:T(8,128)(2,1)}, bf16[2048,512]{0,1:T(8,128)(2,1)}, u32[]{:S(2)}, u32[]{:S(2)}) collective-permute-start(bf16[2048,512]{0,1:T(8,128)(2,1)} %fusion.40), channel_id=1, source_target_pairs={{0,1},{1,2},{2,3},{3,4},{4,5},{5,6},{6,7},{7,8},{8,9},{9,10},{10,1... | collective-permute-start | bytes 6291464 | tf_op jit(solution)/shard_map/ppermute | solution.py:20
  225.4 37.3 %collective-permute-done.7 = bf16[2048,512]{0,1:T(8,128)(2,1)} collective-permute-done((bf16[2048,512]{0,1:T(8,128)(2,1)}, bf16[2048,512]{0,1:T(8,128)(2,1)}, u32[]{:S(2)}, u32[]{:S(2)}) %collective-permute-start.7) | collective-permute-done | bytes 2097184 | tf_op jit(solution)/shard_map/ppermute | solution.py:23
  262.7 3.8 %collective-permute-done.6 = bf16[2048,512]{0,1:T(8,128)(2,1)} collective-permute-done((bf16[2048,512]{0,1:T(8,128)(2,1)}, bf16[2048,512]{0,1:T(8,128)(2,1)}, u32[]{:S(2)}, u32[]{:S(2)}) %collective-permute-start.6) | collective-permute-done | bytes 2097184 | tf_op jit(solution)/shard_map/ppermute | solution.py:20
  266.6 7.5 %fusion.9 = bf16[512,1536]{1,0:T(8,128)(2,1)} fusion(bf16[512,2048]{1,0:T(8,128)(2,1)S(1)} %multiply_convert_fusion, bf16[2048,512]{0,1:T(8,128)(2,1)} %collective-permute-done.7, bf16[2048,512]{0,1:T(8,128)(2,1)} %fusion.40, bf16[2048,512]{0,1:T(8,128)(2,1)} %collective-permute-done.6), kind=kOutput, calls=%fused_computation.13 | convolution fusion | flops 3241672704 | bytes 9961472 | tf_op jit(solution)/shard_map/dot_general | solution.py:54
  (78 shorter events, 48.1 us)
Async XLA Ops:
  0.6 25.8 %collective-permute-start = (bf16[2048,512]{1,0:T(8,128)(2,1)}, bf16[2048,512]{1,0:T(8,128)(2,1)S(1)}, u32[]{:S(2)}, u32[]{:S(2)}) collective-permute-start(bf16[2048,512]{1,0:T(8,128)(2,1)} %param.5), channel_id=1, source_target_pairs={{1,0},{2,1},{3,2},{4,3},{5,4},{6,5},{7,6},{8,7},{9,8},{10,9},{11,1... | collective-permute-start | bytes 6291464 | tf_op jit(solution)/shard_map/ppermute | solution.py:12
  26.4 1.4 copy-start.3
  27.8 27.2 %collective-permute-start.1 = (bf16[2048,512]{1,0:T(8,128)(2,1)S(1)}, bf16[2048,512]{1,0:T(8,128)(2,1)S(1)}, u32[]{:S(2)}, u32[]{:S(2)}) collective-permute-start(bf16[2048,512]{1,0:T(8,128)(2,1)S(1)} %collective-permute-done), channel_id=1, source_target_pairs={{1,0},{2,1},{3,2},{4,3},{5,4},{6,5},{7,6},{8,7},{9,8},{10,9},{11,1... | collective-permute-start | bytes 6291464 | tf_op jit(solution)/shard_map/ppermute | solution.py:12
  55.0 1.3 copy-start.5
  56.3 27.3 %collective-permute-start.2 = (bf16[2048,512]{1,0:T(8,128)(2,1)S(1)}, bf16[2048,512]{1,0:T(8,128)(2,1)S(1)}, u32[]{:S(2)}, u32[]{:S(2)}) collective-permute-start(bf16[2048,512]{1,0:T(8,128)(2,1)S(1)} %collective-permute-done.1), channel_id=1, source_target_pairs={{1,0},{2,1},{3,2},{4,3},{5,4},{6,5},{7,6},{8,7},{9,8},{10,9},{11,1... | collective-permute-start | bytes 6291464 | tf_op jit(solution)/shard_map/ppermute | solution.py:12
  83.7 7.8 %copy-start.7 = (bf16[2048,512]{1,0:T(8,128)(2,1)}, bf16[2048,512]{1,0:T(8,128)(2,1)S(1)}, u32[]{:S(2)}) copy-start(bf16[2048,512]{1,0:T(8,128)(2,1)S(1)} %collective-permute-done.2) | copy-start | bytes 6291460
  83.7 27.3 %collective-permute-start.3 = (bf16[2048,512]{1,0:T(8,128)(2,1)S(1)}, bf16[2048,512]{1,0:T(8,128)(2,1)}, u32[]{:S(2)}, u32[]{:S(2)}) collective-permute-start(bf16[2048,512]{1,0:T(8,128)(2,1)S(1)} %collective-permute-done.2), channel_id=1, source_target_pairs={{1,0},{2,1},{3,2},{4,3},{5,4},{6,5},{7,6},{8,7},{9,8},{10,9},{11,1... | collective-permute-start | bytes 6291464 | tf_op jit(solution)/shard_map/ppermute | solution.py:12
  111.0 63.8 %collective-permute-start.4 = (bf16[2048,512]{1,0:T(8,128)(2,1)}, bf16[2048,512]{1,0:T(8,128)(2,1)}, u32[]{:S(2)}, u32[]{:S(2)}) collective-permute-start(bf16[2048,512]{1,0:T(8,128)(2,1)} %collective-permute-done.3), channel_id=1, source_target_pairs={{1,0},{2,1},{3,2},{4,3},{5,4},{6,5},{7,6},{8,7},{9,8},{10,9},{11,1... | collective-permute-start | bytes 6291464 | tf_op jit(solution)/shard_map/ppermute | solution.py:12
  174.8 27.9 %collective-permute-start.5 = (bf16[2048,512]{1,0:T(8,128)(2,1)}, bf16[2048,512]{1,0:T(8,128)(2,1)S(1)}, u32[]{:S(2)}, u32[]{:S(2)}) collective-permute-start(bf16[2048,512]{1,0:T(8,128)(2,1)} %collective-permute-done.4), channel_id=1, source_target_pairs={{1,0},{2,1},{3,2},{4,3},{5,4},{6,5},{7,6},{8,7},{9,8},{10,9},{11,1... | collective-permute-start | bytes 6291464 | tf_op jit(solution)/shard_map/ppermute | solution.py:12
  178.8 3.2 %copy-start.1 = (bf16[16,32,3584]{2,1,0:T(8,128)(2,1)S(1)}, bf16[16,32,3584]{2,1,0:T(8,128)(2,1)}, u32[]{:S(2)}) copy-start(bf16[16,32,3584]{2,1,0:T(8,128)(2,1)} %get-tuple-element.9) | copy-start | bytes 11010052
  178.8 3.5 %copy-start.4 = (bf16[2048,512]{1,0:T(8,128)(2,1)S(1)}, bf16[2048,512]{1,0:T(8,128)(2,1)}, u32[]{:S(2)}) copy-start(bf16[2048,512]{1,0:T(8,128)(2,1)} %copy-done.3) | copy-start | bytes 6291460
  182.3 1.6 copy-start.6
  183.9 1.6 copy-start.8
  210.0 2.7 copy-start
  210.6 10.1 %copy-start.2 = (f32[2048,32]{0,1:T(8,128)S(1)}, f32[2048,32]{0,1:T(8,128)}, u32[]{:S(2)}) copy-start(f32[2048,32]{0,1:T(8,128)} %param.9) | copy-start | bytes 786436
  212.7 50.0 %collective-permute-start.7 = (bf16[2048,512]{0,1:T(8,128)(2,1)}, bf16[2048,512]{0,1:T(8,128)(2,1)}, u32[]{:S(2)}, u32[]{:S(2)}) collective-permute-start(bf16[2048,512]{0,1:T(8,128)(2,1)} %fusion.40), channel_id=1, source_target_pairs={{1,0},{2,1},{3,2},{4,3},{5,4},{6,5},{7,6},{8,7},{9,8},{10,9},{11,1... | collective-permute-start | bytes 6291464 | tf_op jit(solution)/shard_map/ppermute | solution.py:23
  216.4 50.1 %collective-permute-start.6 = (bf16[2048,512]{0,1:T(8,128)(2,1)}, bf16[2048,512]{0,1:T(8,128)(2,1)}, u32[]{:S(2)}, u32[]{:S(2)}) collective-permute-start(bf16[2048,512]{0,1:T(8,128)(2,1)} %fusion.40), channel_id=1, source_target_pairs={{0,1},{1,2},{2,3},{3,4},{4,5},{5,6},{6,7},{7,8},{8,9},{9,10},{10,1... | collective-permute-start | bytes 6291464 | tf_op jit(solution)/shard_map/ppermute | solution.py:20
where the time goes:
time: 276 us; the launch traced here: 274 us
  waiting for transfers between devices  132 us (48%)
  local copies, waits for them, and re-layouts  68.1 us (25%)
  matrix products  34.2 us (12%)
  starting transfers between devices  29.2 us (11%)
  other arithmetic  9.64 us (3%)
    ppermute x6, waiting for transfers between devices, from_behind(): lax.ppermute(value, axis, [(source, source + steps) for source in range(f...  90.8 us
    gather x48, local copies, waits for them, and re-layouts  59.8 us
    ppermute x1, waiting for transfers between devices, padded_2(): lax.ppermute(lax.slice_in_dim(block, 0, width, axis=dim), axis, backward)  37.3 us
    dot_general x7, matrix products, add_block(): lax.dot_general(incoming, weight_slab, (((1,), (1,)), ((), ())), preferre...  26 us
    ppermute x6, starting transfers between devices, from_behind(): lax.ppermute(value, axis, [(source, source + steps) for source in range(f...  21.2 us
    dot_general x2, matrix products, cross_product(): lax.dot_general(left, right, (((0,), (0,)), ((), ())), preferred_element_...  8.17 us
  transfers between devices with their start and end apart: 8, of which 7 were waited for; matrix products, arithmetic and copies ran while one was open for 33% of the time, Pallas kernels for 0%

commit v1 on v0

v1 whole, which is shorter than its diff:
```python
import functools

import jax
import jax.numpy as jnp
from jax import lax
from jax.experimental import pallas as pl
from jax.experimental.pallas import tpu as pltpu
from jax.sharding import PartitionSpec as P

EPSILON = 1e-05
ROUND = 128
CHUNK = 128
XF, XH, ZF, ZH, PEER = 0, 1, 2, 3, 4


def dot_nt(left, right):
    return lax.dot_general(
        left, right, (((1,), (1,)), ((), ())), preferred_element_type=jnp.float32
    )


def standardize_rows(values):
    scale = 1.0 / values.shape[1]
    centred = values - jnp.sum(values, axis=1, keepdims=True) * scale
    spread = jnp.sum(centred * centred, axis=1, keepdims=True) * scale
    return (centred * lax.rsqrt(spread + EPSILON)).astype(jnp.bfloat16)


def kernel(
    n, starts_ref, ends_ref, geno_hbm, weights_hbm, pheno_ref, scores_ref, link_ref,
    wbuf, gbuf, placed, et, scaled, rx, ret_out, ret_in,
    wsem, gsem, send, recv, fsend, frecv, bsend, brecv,
):
    me = lax.axis_index("var")
    core = lax.rem(me, 2)
    col = lax.rem(lax.div(me, 2), 2)
    other = 1 - core
    genes, tissues, span = weights_hbm.shape
    samples, cols = geno_hbm.shape
    reach = span // cols
    rounds = samples // ROUND
    half = ROUND // 2
    x_peer = me + 2 - 4 * col
    sibling = me + 1 - 2 * core
    up = me + 4 < n
    down = me >= 4
    is_a = col == 0

    def weight_copy(g):
        return pltpu.make_async_copy(weights_hbm.at[g], wbuf.at[g], wsem.at[g])

    own_copy = pltpu.make_async_copy(geno_hbm, gbuf.at[core], gsem)
    own_copy.start()

    barrier = pltpu.get_barrier_semaphore()
    expected = jnp.int32(0)
    for peer in (me - 4, me + 4, me - 1, me + 1):
        exists = jnp.logical_and(peer >= 0, peer < n)
        expected = expected + exists.astype(jnp.int32)

        @pl.when(exists)
        def _():
            pl.semaphore_signal(
                barrier, inc=1, device_id={"var": peer}, device_id_type=pl.DeviceIdType.MESH
            )

    pl.semaphore_signal(
        barrier, inc=1, device_id={"var": x_peer}, device_id_type=pl.DeviceIdType.MESH
    )
    pl.semaphore_wait(barrier, expected + 1)
    own_copy.wait()

    def piece(q, j, s, part):
        if part is None:
            return gbuf.at[2 * q + j, pl.ds(s * ROUND, ROUND), :]
        return gbuf.at[2 * q + j, pl.ds(s * ROUND + part * half, half), :]

    def remote(kind, s, source, target, device):
        return pltpu.make_async_remote_copy(
            src_ref=source,
            dst_ref=target,
            send_sem=send.at[kind, s],
            recv_sem=recv.at[kind, s],
            device_id={"var": device},
            device_id_type=pl.DeviceIdType.MESH,
        )

    def out_copy(kind, s):
        if kind == XF:
            return remote(XF, s, piece(2 - 2 * col, core, s, None), piece(1, core, s, None), x_peer)
        if kind == XH:
            part = 1 - col
            return remote(
                XH, s, piece(3 - col, core, s, part), piece(2 + col, core, s, part), x_peer
            )
        if kind == ZF:
            return remote(ZF, s, piece(col, core, s, None), piece(2 + col, core, s, None), me - 4)
        if kind == ZH:
            part = 1 - col
            return remote(
                ZH, s, piece(1 - col, core, s, part), piece(3 - col, core, s, part), me - 4
            )
        q = kind - PEER + 1 - core
        return remote(kind, s, piece(q, core, s, None), piece(q, core, s, None), sibling)

    def in_copy(kind, s):
        if kind == XF:
            ref = piece(1, core, s, None)
        elif kind == XH:
            ref = piece(3 - col, core, s, col)
        elif kind == ZF:
            ref = piece(2 + col, core, s, None)
        elif kind == ZH:
            ref = piece(3 - col, core, s, 1 - col)
        else:
            ref = piece(kind - PEER + core, other, s, None)
        return remote(kind, s, ref, ref, sibling)

    in_zf = me + 4 + 4 * col < n
    in_xf = jnp.logical_or(is_a, up)
    sends = {
        XF: jnp.logical_or(col == 1, up),
        XH: up,
        ZF: jnp.logical_and(down, jnp.logical_or(is_a, up)),
        ZH: down,
    }
    recvs = {XF: in_xf, XH: up, ZF: in_zf, ZH: up}
    has = [me >= 0, in_xf, up, in_zf]
    for m in range(3):
        sends[PEER + m] = jnp.where(core == 0, has[m + 1], has[m])
        recvs[PEER + m] = jnp.where(core == 0, has[m], has[m + 1])

    def start(kind, s, *conditions):
        ok = sends[kind]
        for condition in conditions:
            ok = jnp.logical_and(ok, condition)

        @pl.when(ok)
        def _():
            out_copy(kind, s).start()

    def arrive(kind, s, *conditions):
        ok = recvs[kind]
        for condition in conditions:
            ok = jnp.logical_and(ok, condition)

        @pl.when(ok)
        def _():
            in_copy(kind, s).wait_recv()

    is_b = col == 1
    first = core == 0
    second = core == 1

    def issue_own(s, carry):
        start(ZF, s, is_a)
        start(XF, s, is_b)
        start(ZH, s, is_b)
        start(PEER, s, second)
        return carry

    lax.fori_loop(0, rounds, issue_own, 0)

    def issue_weights(g, carry):
        weight_copy(g).start()
        return carry

    lax.fori_loop(0, genes, issue_weights, 0)

    base = me * cols
    width = span + cols

    def place(g):
        weight_copy(g).wait()
        offset = starts_ref[g] - base
        stop = ends_ref[g] - base
        padded = jnp.concatenate(
            [wbuf[g], jnp.zeros((tissues, cols), jnp.float32)], axis=1
        )
        moved = pltpu.roll(padded, offset, 1)
        column = lax.broadcasted_iota(jnp.int32, (tissues, width), 1)
        inside = jnp.logical_and(column >= offset, column < stop)
        placed[pl.ds(g * tissues, tissues), :] = jnp.where(inside, moved, 0.0).astype(
            jnp.bfloat16
        )

    def relay_one(s, carry):
        arrive(ZF, s, is_a)
        start(XF, s, is_a)
        arrive(XF, s)
        start(ZH, s, is_a)
        start(ZF, s, is_b)
        start(PEER, s, first)
        start(PEER + 1, s, second)
        arrive(ZH, s, is_b)
        start(XH, s, is_b)
        start(PEER + 1, s, first, is_a)
        start(PEER + 2, s, second, is_a)
        return carry

    per_round = -(-genes // rounds)

    def first_stage(s, carry):
        relay_one(s, 0)
        for extra in range(per_round):
            g = s * per_round + extra

            @pl.when(g < genes)
            def _():
                place(g)

        return carry

    lax.fori_loop(0, rounds, first_stage, 0)

    def multiply(pair):
        rows = pl.ds(pair * 2 * ROUND, 2 * ROUND)
        for d in range(reach + 1):

            @pl.when(me + d < n)
            def _():
                product = dot_nt(placed[:, d * cols : (d + 1) * cols], gbuf[core + d, rows, :])
                if d == 0:
                    et[:, rows] = product
                else:
                    et[:, rows] += product

    def second_stage(s, carry):
        @pl.when(s < rounds)
        def _():
            arrive(ZH, s, is_a)
            start(XH, s, is_a)
            arrive(XH, s)
            start(PEER + 1, s, first, is_b)
            start(PEER + 2, s, second, is_b)
            arrive(ZF, s, is_b)
            start(PEER + 2, s, first)

        @pl.when(jnp.logical_and(s >= 2, lax.rem(s, 2) == 0))
        def _():
            for back in (2, 1):
                for m in range(3):
                    arrive(PEER + m, s - back)
            multiply(lax.div(s, 2) - 1)

        return carry

    lax.fori_loop(0, rounds + 1, second_stage, 0)

    total = placed.shape[0]
    chunks = total // CHUNK
    has_next = me < n - 1
    has_prev = me > 0

    def forward(c):
        rows = pl.ds(c * CHUNK, CHUNK)
        return pltpu.make_async_remote_copy(
            src_ref=scaled.at[rows, :],
            dst_ref=rx.at[rows, :],
            send_sem=fsend.at[c],
            recv_sem=frecv.at[c],
            device_id={"var": me + 1},
            device_id_type=pl.DeviceIdType.MESH,
        )

    def backward(c):
        rows = pl.ds(c * CHUNK, CHUNK)
        return pltpu.make_async_remote_copy(
            src_ref=ret_out.at[rows, :],
            dst_ref=ret_in.at[rows, :],
            send_sem=bsend.at[c],
            recv_sem=brecv.at[c],
            device_id={"var": me - 1},
            device_id_type=pl.DeviceIdType.MESH,
        )

    step = 32

    def standardize_chunk(c, carry):
        def some(b, inner):
            rows = pl.ds(c * CHUNK + b * step, step)
            scaled[rows, :] = standardize_rows(et[rows, :])
            return inner

        lax.fori_loop(0, CHUNK // step, some, 0)

        @pl.when(has_next)
        def _():
            forward(c).start()

        return carry

    lax.fori_loop(0, chunks, standardize_chunk, 0)

    shrink = 1.0 / samples
    pheno_scaled = standardize_rows(pheno_ref[...])
    scores_ref[...] = dot_nt(scaled[...], pheno_scaled) / jnp.sqrt(jnp.float32(samples))

    def own_block(c, carry):
        rows = pl.ds(c * CHUNK, CHUNK)
        link_ref[rows, total : 2 * total] = (dot_nt(scaled[rows, :], scaled[...]) * shrink).astype(
            jnp.bfloat16
        )
        return carry

    lax.fori_loop(0, chunks, own_block, 0)

    def before(c, carry):
        rows = pl.ds(c * CHUNK, CHUNK)

        @pl.when(has_prev)
        def _():
            forward(c).wait_recv()
            product = (dot_nt(rx[rows, :], scaled[...]) * shrink).astype(jnp.bfloat16)
            ret_out[rows, :] = product
            across = (dot_nt(scaled[...], rx[rows, :]) * shrink).astype(jnp.bfloat16)
            link_ref[:, pl.ds(pl.multiple_of(c * CHUNK, CHUNK), CHUNK)] = across
            backward(c).start()

        return carry

    lax.fori_loop(0, chunks, before, 0)

    @pl.when(jnp.logical_not(has_prev))
    def _():
        link_ref[:, :total] = jnp.zeros((total, total), jnp.bfloat16)

    @pl.when(jnp.logical_not(has_next))
    def _():
        link_ref[:, 2 * total :] = jnp.zeros((total, total), jnp.bfloat16)

    def drain(s, carry):
        for kind in range(PEER + 3):

            @pl.when(sends[kind])
            def _():
                out_copy(kind, s).wait_send()

        return carry

    lax.fori_loop(0, rounds, drain, 0)

    def after(c, carry):
        rows = pl.ds(c * CHUNK, CHUNK)

        @pl.when(has_next)
        def _():
            backward(c).wait_recv()
            link_ref[rows, 2 * total :] = ret_in[rows, :]
            forward(c).wait_send()

        @pl.when(has_prev)
        def _():
            backward(c).wait_send()

        return carry

    lax.fori_loop(0, chunks, after, 0)


def on_device(n, genotypes, weights, starts, ends, phenotypes):
    samples, cols = genotypes.shape
    genes, tissues, span = weights.shape
    total = genes * tissues
    slots = span // cols + 2
    rounds = samples // ROUND
    chunks = total // CHUNK
    vmem = pl.BlockSpec(memory_space=pltpu.VMEM)
    smem = pl.BlockSpec(memory_space=pltpu.SMEM)
    hbm = pl.BlockSpec(memory_space=pl.ANY)
    dma = pltpu.SemaphoreType.DMA
    traits = phenotypes.shape[1]
    scores, linkage = pl.pallas_call(
        functools.partial(kernel, n),
        out_shape=(
            jax.ShapeDtypeStruct((total, traits), jnp.float32),
            jax.ShapeDtypeStruct((total, 3 * total), jnp.bfloat16),
        ),
        in_specs=[smem, smem, hbm, hbm, vmem],
        out_specs=(vmem, vmem),
        scratch_shapes=[
            pltpu.VMEM((genes, tissues, span), jnp.float32),
            pltpu.VMEM((slots, samples, cols), jnp.bfloat16),
            pltpu.VMEM((total, span + cols), jnp.bfloat16),
            pltpu.VMEM((total, samples), jnp.float32),
            pltpu.VMEM((total, samples), jnp.bfloat16),
            pltpu.VMEM((total, samples), jnp.bfloat16),
            pltpu.VMEM((total, total), jnp.bfloat16),
            pltpu.VMEM((total, total), jnp.bfloat16),
            dma((genes,)),
            dma,
            dma((PEER + 3, rounds)),
            dma((PEER + 3, rounds)),
            dma((chunks,)),
            dma((chunks,)),
            dma((chunks,)),
            dma((chunks,)),
        ],
        compiler_params=pltpu.CompilerParams(
            collective_id=0, has_side_effects=True, vmem_limit_bytes=60 * 1024 * 1024
        ),
    )(starts, ends, genotypes, weights, phenotypes.T)
    return scores.reshape(genes, -1), linkage


def solution(mesh):
    placed = (
        P(None, ("chrom", "var")),
        P(("chrom", "var"), None, None),
        P(("chrom", "var")),
        P(("chrom", "var")),
        P(),
    )
    return jax.shard_map(
        functools.partial(on_device, mesh.shape["var"]),
        mesh=mesh,
        in_specs=placed,
        out_specs=(P(("chrom", "var"), None), P(("chrom", "var"), None)),
        check_vma=False,
    )
```

time: 276 us -> 126 us (0.46)
  waiting for transfers between devices: 132 us -> 0 us
  Pallas kernels: 0 us -> 119 us
  local copies, waits for them, and re-layouts: 68.1 us -> 4.37 us
  matrix products: 34.2 us -> 0 us
  starting transfers between devices: 29.2 us -> 0 us
  other arithmetic: 9.64 us -> 0 us
    ppermute x8 -> x0, waiting for transfers between devices: 132 us -> none  [the longest x6 90.8 us: from_behind(): lax.ppermute(value, axis, [(source, source + steps) for source in range(f...]
    pallas_call x0 -> x1, Pallas kernels: none -> 119 us  [on_device(): pl.pallas_call(functools.partial(kernel, n), out_shape=(jax.ShapeDtypeStr...]
    gather x48 -> x0, local copies, waits for them, and re-layouts: 59.8 us -> none
    dot_general x9 -> x0, matrix products: 34.2 us -> none  [the longest x7 26 us: add_block(): lax.dot_general(incoming, weight_slab, (((1,), (1,)), ((), ())), preferre...]
    ppermute x8 -> x0, starting transfers between devices: 29.2 us -> none  [the longest x6 21.2 us: from_behind(): lax.ppermute(value, axis, [(source, source + steps) for source in range(f...]
    convert_element_type x2 -> x0, other arithmetic: 4.75 us -> none  [standardize(): return (centred * lax.rsqrt(spread + EPSILON)).astype(jnp.bfloat16)]
    pad x1 -> x0, local copies, waits for them, and re-layouts: 3.82 us -> none  [place_weights(): jnp.pad(masked, ((0, 0), (0, 0), (window_cols, window_cols - span)))]
    select_n x1 -> x0, other arithmetic: 3.19 us -> none  [place_weights(): jnp.where(column[None, None, :] < lengths[:, None, None], rounded, jnp.ze...]
  transfers between devices with their start and end apart: 8 -> 0, of which waited for: 7 -> 0; matrix products, arithmetic and copies ran while one was open for 33% -> 0% of each run, Pallas kernels for 0% -> 0%
where the time goes in v1:
time: 126 us; the launch traced here: 124 us
  Pallas kernels  119 us (94%)
  local copies, waits for them, and re-layouts  4.37 us (3%)
    pallas_call x1, Pallas kernels, on_device(): pl.pallas_call(functools.partial(kernel, n), out_shape=(jax.ShapeDtypeStr...  119 us
    unnamed x1, local copies, waits for them, and re-layouts  2.65 us

profile of v1, /device:TPU:18, one launch (start us, length us, event | category | flops | bytes accessed | tf_op | source)
XLA Modules:
  0.0 123.5 jit_solution(8259851385461228700)
XLA Ops:
  0.6 118.5 %shard_map.68 = (f32[512,32]{1,0:T(8,128)}, bf16[512,1536]{1,0:T(8,128)(2,1)}) custom-call(s32[16]{0:T(128)} %starts_ref.1, s32[16]{0:T(128)} %ends_ref.1, bf16[2048,512]{1,0:T(8,128)(2,1)} %geno_hbm.1, f32[16,32,3072]{2,1,0:T(8,128)} %weights_hbm.1, f32[32,2048]{1,0:T(8,128)} %bitcast.1), custom_call_target="tpu_custom_call" | custom-call | tf_op jit(solution)/shard_map/pallas_call | solution.py:373
  119.1 1.7 %reshape.7 = f32[16,1024]{1,0:T(8,128)} reshape(f32[512,32]{1,0:T(8,128)} %get-tuple-element.4) | data formatting | bytes 131072 | tf_op jit(solution)/shard_map/reshape | solution.py:403
  120.9 2.7 %copy.8 = bf16[512,1536]{1,0:T(8,128)(2,1)} copy(bf16[512,1536]{1,0:T(8,128)(2,1)} %get-tuple-element.9) | data formatting | bytes 3145728

commit v2 on v1

--- a/solution.py
+++ b/solution.py
@@ -9,7 +9,8 @@
 
 EPSILON = 1e-05
 ROUND = 128
-CHUNK = 128
+PRODUCT = 256
+CHUNK = 64
 XF, XH, ZF, ZH, PEER = 0, 1, 2, 3, 4
 
 
@@ -161,6 +162,18 @@
 
     lax.fori_loop(0, rounds, issue_own, 0)
 
+    for q in range(1, gbuf.shape[0] // 2):
+
+        @pl.when(jnp.logical_not(has[q]))
+        def _():
+            def clear(s, carry):
+                gbuf[2 * q : 2 * q + 2, pl.ds(s * ROUND, ROUND), :] = jnp.zeros(
+                    (2, ROUND, cols), gbuf.dtype
+                )
+                return carry
+
+            lax.fori_loop(0, rounds, clear, 0)
+
     def issue_weights(g, carry):
         weight_copy(g).start()
         return carry
@@ -214,16 +227,13 @@
     lax.fori_loop(0, rounds, first_stage, 0)
 
     def multiply(pair):
-        rows = pl.ds(pair * 2 * ROUND, 2 * ROUND)
-        for d in range(reach + 1):
-
-            @pl.when(me + d < n)
-            def _():
-                product = dot_nt(placed[:, d * cols : (d + 1) * cols], gbuf[core + d, rows, :])
-                if d == 0:
-                    et[:, rows] = product
-                else:
-                    et[:, rows] += product
+        rows = pl.ds(pair * PRODUCT, PRODUCT)
+        acc = dot_nt(placed[:, :cols], gbuf[core, rows, :])
+        for d in range(1, reach + 1):
+            acc = acc + dot_nt(placed[:, d * cols : (d + 1) * cols], gbuf[core + d, rows, :])
+        et[:, rows] = acc
+
+    group = PRODUCT // ROUND
 
     def second_stage(s, carry):
         @pl.when(s < rounds)
@@ -236,12 +246,12 @@
             arrive(ZF, s, is_b)
             start(PEER + 2, s, first)
 
-        @pl.when(jnp.logical_and(s >= 2, lax.rem(s, 2) == 0))
-        def _():
-            for back in (2, 1):
+        @pl.when(jnp.logical_and(s >= group, lax.rem(s, group) == 0))
+        def _():
+            for back in range(group, 0, -1):
                 for m in range(3):
                     arrive(PEER + m, s - back)
-            multiply(lax.div(s, 2) - 1)
+            multiply(lax.div(s, group) - 1)
 
         return carry
 
@@ -313,13 +323,15 @@
             forward(c).wait_recv()
             product = (dot_nt(rx[rows, :], scaled[...]) * shrink).astype(jnp.bfloat16)
             ret_out[rows, :] = product
-            across = (dot_nt(scaled[...], rx[rows, :]) * shrink).astype(jnp.bfloat16)
-            link_ref[:, pl.ds(pl.multiple_of(c * CHUNK, CHUNK), CHUNK)] = across
             backward(c).start()
 
         return carry
 
     lax.fori_loop(0, chunks, before, 0)
+
+    @pl.when(has_prev)
+    def _():
+        link_ref[:, :total] = (dot_nt(scaled[...], rx[...]) * shrink).astype(jnp.bfloat16)
 
     @pl.when(jnp.logical_not(has_prev))
     def _():

time: 126 us -> 119 us (0.944)
  Pallas kernels: 119 us -> 112 us
    pallas_call x1, Pallas kernels: 119 us -> 112 us  [on_device(): pl.pallas_call(functools.partial(kernel, n), out_shape=(jax.ShapeDtypeStr...]
where the time goes in v2:
time: 119 us; the launch traced here: 117 us
  Pallas kernels  112 us (94%)
  local copies, waits for them, and re-layouts  4.37 us (4%)
    pallas_call x1, Pallas kernels, on_device(): pl.pallas_call(functools.partial(kernel, n), out_shape=(jax.ShapeDtypeStr...  112 us
    unnamed x1, local copies, waits for them, and re-layouts  2.65 us

profile of v2, /device:TPU:18, one launch (start us, length us, event | category | flops | bytes accessed | tf_op | source)
XLA Modules:
  0.0 117.3 jit_solution(9608247766952195058)
XLA Ops:
  0.6 112.3 %shard_map.68 = (f32[512,32]{1,0:T(8,128)}, bf16[512,1536]{1,0:T(8,128)(2,1)}) custom-call(s32[16]{0:T(128)} %starts_ref.1, s32[16]{0:T(128)} %ends_ref.1, bf16[2048,512]{1,0:T(8,128)(2,1)} %geno_hbm.1, f32[16,32,3072]{2,1,0:T(8,128)} %weights_hbm.1, f32[32,2048]{1,0:T(8,128)} %bitcast.1), custom_call_target="tpu_custom_call" | custom-call | tf_op jit(solution)/shard_map/pallas_call | solution.py:385
  112.9 1.7 %reshape.7 = f32[16,1024]{1,0:T(8,128)} reshape(f32[512,32]{1,0:T(8,128)} %get-tuple-element.4) | data formatting | bytes 131072 | tf_op jit(solution)/shard_map/reshape | solution.py:415
  114.6 2.7 %copy.8 = bf16[512,1536]{1,0:T(8,128)(2,1)} copy(bf16[512,1536]{1,0:T(8,128)(2,1)} %get-tuple-element.9) | data formatting | bytes 3145728
